TPU v7x, 32 devices: a whole 2x2x4 slice. The times are simulated.
32 devices in a mesh: owner: 4 (over y, x), rows: 8 (over z, core).
Axes of the slice: x: 2, y: 2, z: 4, core: 2. Of those that a mesh axis runs over, the one named last changes fastest.
Arguments:
- train_gate: float32 [64, 2048, 1024], P('owner', 'rows'), may hold values from -0.1875 to 0.1875
- train_up: float32 [64, 2048, 1024], P('owner', 'rows'), may hold values from -0.1875 to 0.1875
- train_down: float32 [64, 1024, 2048], P('owner', None, 'rows'), may hold values from -0.25 to 0.25
- router_weight: float32 [2048, 64], P('rows', 'owner'), may hold values from -0.125 to 0.125
- router_gain: float32 [2048], P('rows'), may hold values from 0.25 to 1.75
Outputs:
- ready_gate: bfloat16 [64, 2048, 1024], P('owner', None, 'rows')
- ready_up: bfloat16 [64, 2048, 1024], P('owner', None, 'rows')
- ready_down: bfloat16 [64, 1024, 2048], P('owner', 'rows')
- scale_gate: float32 [64, 1024], P('owner', 'rows')
- scale_up: float32 [64, 1024], P('owner', 'rows')
- scale_down: float32 [64, 1024], P('owner', 'rows')
- serve_router: bfloat16 [2048, 64], replicated
All inputs are finite; a program needn't handle non-finite values. Where the computation divides by a largest or mean magnitude, that divisor is 1e-20 or more.
Results may differ from a plain program's by a relative error of at most 0.0013.
Values may be sent and summed in bfloat16 or wider, within the bound.
A program may use at most 192 MiB of HBM per device.

v0:
```python
import jax
import jax.numpy as jnp
from jax import lax
from jax.sharding import PartitionSpec as P

D_MODEL = 2048


def local(train_gate, train_up, train_down, router_weight, router_gain):
    total_gate, total_up, total_down = lax.psum(
        (
            jnp.sum(jnp.abs(train_gate), axis=1),
            jnp.sum(jnp.abs(train_up), axis=1),
            jnp.sum(jnp.abs(train_down), axis=2),
        ),
        "rows",
    )
    scale_gate = total_gate / D_MODEL
    scale_up = total_up / D_MODEL
    scale_down = total_down / D_MODEL
    narrow_gate, narrow_up, narrow_down = (
        (train_gate / jnp.expand_dims(scale_gate, 1)).astype(jnp.bfloat16),
        (train_up / jnp.expand_dims(scale_up, 1)).astype(jnp.bfloat16),
        (train_down / jnp.expand_dims(scale_down, 2)).astype(jnp.bfloat16),
    )
    ready_gate, ready_up = (
        lax.all_to_all(narrow_gate, "rows", split_axis=2, concat_axis=1, tiled=True),
        lax.all_to_all(narrow_up, "rows", split_axis=2, concat_axis=1, tiled=True),
    )
    ready_down = lax.all_to_all(narrow_down, "rows", split_axis=1, concat_axis=2, tiled=True)
    scale_gate = lax.dynamic_slice_in_dim(
        scale_gate, lax.axis_index("rows") * ready_gate.shape[2], ready_gate.shape[2], axis=1
    )
    scale_up = lax.dynamic_slice_in_dim(
        scale_up, lax.axis_index("rows") * ready_up.shape[2], ready_up.shape[2], axis=1
    )
    scale_down = lax.dynamic_slice_in_dim(
        scale_down, lax.axis_index("rows") * ready_down.shape[1], ready_down.shape[1], axis=1
    )
    part_router = (router_weight * router_gain[:, None]).astype(jnp.bfloat16)
    row_router = lax.all_gather(part_router, "rows", axis=0, tiled=True)
    serve_router = lax.all_gather(row_router, "owner", axis=1, tiled=True)
    return (ready_gate, ready_up, ready_down, scale_gate, scale_up, scale_down, serve_router)


def solution(mesh):
    return jax.shard_map(
        local,
        mesh=mesh,
        in_specs=(
            P("owner", "rows", None),
            P("owner", "rows", None),
            P("owner", None, "rows"),
            P("rows", "owner"),
            P("rows"),
        ),
        out_specs=(
            P("owner", None, "rows"),
            P("owner", None, "rows"),
            P("owner", "rows", None),
            P("owner", "rows"),
            P("owner", "rows"),
            P("owner", "rows"),
            P(),
        ),
        check_vma=False,
    )
```

profile of v0, /device:TPU:0, one launch (start us, length us, event | category | flops | bytes accessed | tf_op | source)
XLA Modules:
  0.0 737.8 jit_solution(7608499507201470121)
XLA Ops:
  7.2 8.6 %abs_reduce_fusion = f32[16,1024]{1,0:T(8,128)} fusion(f32[16,1024,256]{2,1,0:T(8,128)} %param.7), kind=kLoop, calls=%fused_computation.2 | loop fusion | flops 8372224 | bytes 16842752 | tf_op jit(solution)/shard_map/reduce_sum | solution.py:14
  15.8 12.6 %abs_reduce_fusion.1 = (f32[16,1024]{1,0:T(8,128)}, f32[16,1024]{1,0:T(8,128)}) fusion(f32[16,256,1024]{2,1,0:T(8,128)} %param.6, f32[16,256,1024]{2,1,0:T(8,128)} %param.5), kind=kLoop, calls=%fused_computation.4 | loop fusion | flops 16744448 | bytes 33685504 | tf_op jit(solution)/shard_map/reduce_sum | solution.py:13
  28.4 17.6 %copy.19 = f32[16,256,1024]{1,0,2:T(8,128)} copy(f32[16,256,1024]{2,1,0:T(8,128)} %param.6) | data formatting | bytes 33554432 | tf_op args[1]
  46.1 40.7 %all-reduce.3.cloned.1.call-done = (f32[16,1024]{1,0:T(8,128)}, f32[16,1024]{1,0:T(8,128)}, f32[16,1024]{1,0:T(8,128)}) async-done(((f32[16,1024]{1,0:T(8,128)}, f32[16,1024]{1,0:T(8,128)}, f32[16,1024]{1,0:T(8,128)}), (f32[16,1024]{1,0:T(8,128)}, f32[16,1024]{1,0:T(8,128)}, f32[16,1024]{1,0:T(8,128)})) %all-reduce.3.cloned.1.call-update) | async-done | bytes 196624 | tf_op jit(solution)/shard_map/psum | solution.py:10
  86.8 0.8 broadcast_multiply_fusion.1
  87.8 9.6 %divide_convert_fusion = bf16[16,256,1024]{1,0,2:T(8,128)(2,1)} fusion(f32[16,256,1024]{1,0,2:T(8,128)} %copy.19, f32[16,1024]{0,1:T(8,128)S(1)} %copy.18), kind=kLoop, calls=%fused_computation.3 | loop fusion | flops 8388608 | bytes 25231360 | tf_op jit(solution)/shard_map/convert_element_type | solution.py:23
  97.5 4.9 all-to-all-start.1
  102.4 17.6 %copy.16 = f32[16,256,1024]{1,0,2:T(8,128)} copy(f32[16,256,1024]{2,1,0:T(8,128)} %param.5) | data formatting | bytes 33554432 | tf_op args[0]
  120.3 9.7 %divide_convert_fusion.1 = bf16[16,256,1024]{1,0,2:T(8,128)(2,1)} fusion(f32[16,256,1024]{1,0,2:T(8,128)} %copy.16, f32[16,1024]{0,1:T(8,128)S(1)} %copy.15), kind=kLoop, calls=%fused_computation.5 | loop fusion | flops 8388608 | bytes 25231360 | tf_op jit(solution)/shard_map/convert_element_type | solution.py:22
  129.9 156.3 %all-to-all-done.1 = bf16[16,256,1024]{1,0,2:T(8,128)(2,1)} async-done(((bf16[16,256,1024]{1,0,2:T(8,128)(2,1)}), bf16[16,256,1024]{1,0,2:T(8,128)(2,1)}, u32[]{:S(2)}, u32[]{:S(2)}) %all-to-all-start.1) | async-done | bytes 8388640 | tf_op jit(solution)/shard_map/all_to_all | solution.py:28
  286.3 4.9 all-to-all-start
  291.5 16.6 %fusion = bf16[16,1024,256]{2,0,1:T(8,128)(2,1)} fusion(f32[16,1024,256]{2,1,0:T(8,128)} %param.7, f32[16,1024]{0,1:T(8,128)S(1)} %copy.21), kind=kLoop, calls=%fused_computation.1 | loop fusion | flops 8388608 | bytes 25231360 | tf_op jit(solution)/shard_map/convert_element_type | solution.py:24
  308.1 167.0 %all-to-all-done = bf16[16,256,1024]{1,0,2:T(8,128)(2,1)} async-done(((bf16[16,256,1024]{1,0,2:T(8,128)(2,1)}), bf16[16,256,1024]{1,0,2:T(8,128)(2,1)}, u32[]{:S(2)}, u32[]{:S(2)}) %all-to-all-start) | async-done | bytes 8388640 | tf_op jit(solution)/shard_map/all_to_all | solution.py:27
  475.1 5.0 all-to-all-start.2
  480.1 189.9 %all_gather.6 = bf16[2048,16]{0,1:T(8,128)(2,1)S(1)} all-gather(bf16[256,16]{0,1:T(8,128)(2,1)S(1)} %multiply_convert_fusion), channel_id=1, replica_groups=mesh['owner'=4,'rows'=8] {'rows'}, dimensions={0}, use_global_device_ids=true | all-gather | bytes 73728 | tf_op jit(solution)/shard_map/all_gather | solution.py:41
  670.0 9.1 %all_gather.7 = bf16[2048,64]{0,1:T(8,128)(2,1)S(1)} all-gather(bf16[2048,16]{0,1:T(8,128)(2,1)S(1)} %all_gather.6), channel_id=1, replica_groups=mesh['owner'=4,'rows'=8] {'owner'}, dimensions={1}, use_global_device_ids=true | all-gather | bytes 327680 | tf_op jit(solution)/shard_map/all_gather | solution.py:42
  679.1 0.6 constant_dynamic-slice_fusion
  679.7 0.6 constant_dynamic-slice_fusion.1
  680.3 0.6 constant_dynamic-slice_fusion.2
  680.9 12.3 %copy.20 = bf16[16,8,256,128]{3,2,1,0:T(8,128)(2,1)} copy(bf16[16,8,256,128]{2,0,3,1:T(8,128)(2,1)} %bitcast.4) | data formatting | bytes 16777216 | tf_op jit(solution)/shard_map/all_to_all | solution.py:28
  693.2 12.3 %copy.17 = bf16[16,8,256,128]{3,2,1,0:T(8,128)(2,1)} copy(bf16[16,8,256,128]{2,0,3,1:T(8,128)(2,1)} %bitcast.1) | data formatting | bytes 16777216 | tf_op jit(solution)/shard_map/all_to_all | solution.py:27
  705.5 11.4 %copy.23 = bf16[16,128,8,256]{3,2,1,0:T(8,128)(2,1)} copy(bf16[16,128,8,256]{3,0,1,2:T(8,128)(2,1)} %bitcast.7) | data formatting | bytes 16777216 | tf_op jit(solution)/shard_map/all_to_all | solution.py:30
  716.9 13.4 %all_to_all.50 = bf16[16,128,2048]{2,1,0:T(8,128)(2,1)} reshape(bf16[16,128,8,256]{3,2,1,0:T(8,128)(2,1)} %copy.23) | data formatting | bytes 16777216 | tf_op jit(solution)/shard_map/all_to_all | solution.py:30
  730.3 0.7 copy.31
  (17 shorter events, 0.7 us)
Async XLA Ops:
  7.2 79.6 %all-reduce.3.cloned.1.call-start = ((), (), s32[]{:S(2)}) async-start(), calls=%async_computation.3 | async-start | bytes 393216 | tf_op jit(solution)/shard_map/psum | solution.py:10
  97.5 188.8 %all-to-all-start.1 = ((bf16[16,256,1024]{1,0,2:T(8,128)(2,1)}), bf16[16,256,1024]{1,0,2:T(8,128)(2,1)}, u32[]{:S(2)}, u32[]{:S(2)}) async-start(bf16[16,256,1024]{1,0,2:T(8,128)(2,1)} %divide_convert_fusion), calls=%async_computation.1 | async-start | bytes 16777216 | tf_op jit(solution)/shard_map/all_to_all | solution.py:28
  102.4 17.6 %copy-start.1 = (f32[16,1024]{1,0:T(8,128)S(1)}, f32[16,1024]{1,0:T(8,128)}, u32[]{:S(2)}) copy-start(f32[16,1024]{1,0:T(8,128)} %get-tuple-element.7) | copy-start | bytes 196612
  120.2 171.0 %copy-start = (f32[16,1024]{1,0:T(8,128)S(1)}, f32[16,1024]{1,0:T(8,128)}, u32[]{:S(2)}) copy-start(f32[16,1024]{1,0:T(8,128)} %get-tuple-element.9) | copy-start | bytes 196612
  286.3 188.8 %all-to-all-start = ((bf16[16,256,1024]{1,0,2:T(8,128)(2,1)}), bf16[16,256,1024]{1,0,2:T(8,128)(2,1)}, u32[]{:S(2)}, u32[]{:S(2)}) async-start(bf16[16,256,1024]{1,0,2:T(8,128)(2,1)} %divide_convert_fusion.1), calls=%async_computation | async-start | bytes 16777216 | tf_op jit(solution)/shard_map/all_to_all | solution.py:27
  291.4 188.7 %copy-start.2 = (f32[256,16]{0,1:T(8,128)S(1)}, f32[256,16]{0,1:T(8,128)}, u32[]{:S(2)}) copy-start(f32[256,16]{0,1:T(8,128)} %param.8) | copy-start | bytes 49156
  291.4 188.7 %copy-start.3 = (f32[256]{0:T(256)S(1)}, f32[256]{0:T(256)}, u32[]{:S(2)}) copy-start(f32[256]{0:T(256)} %param.9) | copy-start | bytes 3076
  475.1 230.4 %all-to-all-start.2 = ((bf16[16,1024,256]{2,0,1:T(8,128)(2,1)}), bf16[16,1024,256]{2,0,1:T(8,128)(2,1)}, u32[]{:S(2)}, u32[]{:S(2)}) async-start(bf16[16,1024,256]{2,0,1:T(8,128)(2,1)} %fusion), calls=%async_computation.2 | async-start | bytes 16777216 | tf_op jit(solution)/shard_map/all_to_all | solution.py:30
Sparse Core Ops, SparseCore 0:
  28.6 58.1 all-reduce.2
where the time goes:
time: 740 us; the launch traced here: 738 us
  waiting for transfers between devices  364 us (49%)
  blocking collectives  199 us (27%)
  local copies, waits for them, and re-layouts  87.7 us (12%)
  other arithmetic  58 us (8%)
  starting transfers between devices  14.9 us (2%)
  between operations  14.2 us (2%)
    all_gather x1, blocking collectives, local(): row_router = lax.all_gather(part_router, 'rows', axis=0, tiled=True)  190 us
    all_to_all x1, waiting for transfers between devices, local(): lax.all_to_all(narrow_gate, 'rows', split_axis=2, concat_axis=1, tiled=True)  167 us
    all_to_all x1, waiting for transfers between devices, local(): lax.all_to_all(narrow_up, 'rows', split_axis=2, concat_axis=1, tiled=True)  156 us
    psum x1, waiting for transfers between devices, local(): lax.psum((jnp.sum(jnp.abs(train_gate), axis=1), jnp.sum(jnp.abs(train_up)...  40.7 us
    unnamed x11, local copies, waits for them, and re-layouts  36 us
    all_to_all x2, local copies, waits for them, and re-layouts, local(): lax.all_to_all(narrow_down, 'rows', split_axis=1, concat_axis=2, tiled=True)  24.8 us
    convert_element_type x1, other arithmetic, local(): (train_down / jnp.expand_dims(scale_down, 2)).astype(jnp.bfloat16)  16.6 us
  transfers between devices with their start and end apart: 4, of which 3 were waited for; matrix products, arithmetic and copies ran while one was open for 12% of the time, Pallas kernels for 0%

commit v1 on v0

--- a/solution.py
+++ b/solution.py
@@ -39,7 +39,9 @@
     )
     part_router = (router_weight * router_gain[:, None]).astype(jnp.bfloat16)
     row_router = lax.all_gather(part_router, "rows", axis=0, tiled=True)
-    serve_router = lax.all_gather(row_router, "owner", axis=1, tiled=True)
+    serve_router = jnp.concatenate(
+        lax.all_to_all(jnp.stack([row_router] * lax.axis_size("owner")), "owner", 0, 0), axis=1
+    )
     return (ready_gate, ready_up, ready_down, scale_gate, scale_up, scale_down, serve_router)
 
 

time: 740 us -> 698 us (0.943)
  blocking collectives: 199 us -> 15.7 us
  waiting for transfers between devices: 364 us -> 501 us
    all_gather x1, blocking collectives: 190 us -> 15.7 us  [local(): row_router = lax.all_gather(part_router, 'rows', axis=0, tiled=True)]
    all_to_all x1, waiting for transfers between devices: 0.01 us -> 157 us  [local(): lax.all_to_all(narrow_down, 'rows', split_axis=1, concat_axis=2, tiled=True)]
    psum x1, waiting for transfers between devices: 40.7 us -> 20.6 us  [local(): lax.psum((jnp.sum(jnp.abs(train_gate), axis=1), jnp.sum(jnp.abs(train_up)...]
    all_gather x1 -> x0, blocking collectives: 9.11 us -> none  [local(): serve_router = lax.all_gather(row_router, 'owner', axis=1, tiled=True)]
  transfers between devices with their start and end apart: 4 -> 5, of which waited for: 3 -> 4; matrix products, arithmetic and copies ran while one was open for 12% -> 14% of each run, Pallas kernels for 0% -> 0%
where the time goes in v1:
time: 698 us; the launch traced here: 696 us
  waiting for transfers between devices  501 us (72%)
  local copies, waits for them, and re-layouts  88.4 us (13%)
  other arithmetic  58 us (8%)
  starting transfers between devices  18.9 us (3%)
  blocking collectives  15.7 us (2%)
  between operations  14.2 us (2%)
    all_to_all x1, waiting for transfers between devices, local(): lax.all_to_all(narrow_gate, 'rows', split_axis=2, concat_axis=1, tiled=True)  167 us
    all_to_all x1, waiting for transfers between devices, local(): lax.all_to_all(narrow_down, 'rows', split_axis=1, concat_axis=2, tiled=True)  157 us
    all_to_all x1, waiting for transfers between devices, local(): lax.all_to_all(narrow_up, 'rows', split_axis=2, concat_axis=1, tiled=True)  156 us
    unnamed x11, local copies, waits for them, and re-layouts  35.9 us
    all_to_all x2, local copies, waits for them, and re-layouts, local(): lax.all_to_all(narrow_down, 'rows', split_axis=1, concat_axis=2, tiled=True)  24.8 us
    psum x1, waiting for transfers between devices, local(): lax.psum((jnp.sum(jnp.abs(train_gate), axis=1), jnp.sum(jnp.abs(train_up)...  20.6 us
    convert_element_type x1, other arithmetic, local(): (train_down / jnp.expand_dims(scale_down, 2)).astype(jnp.bfloat16)  16.6 us
    all_gather x1, blocking collectives, local(): row_router = lax.all_gather(part_router, 'rows', axis=0, tiled=True)  15.7 us
  transfers between devices with their start and end apart: 5, of which 4 were waited for; matrix products, arithmetic and copies ran while one was open for 14% of the time, Pallas kernels for 0%

profile of v1, /device:TPU:0, one launch (start us, length us, event | category | flops | bytes accessed | tf_op | source)
XLA Modules:
  0.0 696.4 jit_solution(16060710128545141370)
XLA Ops:
  7.2 8.6 %abs_reduce_fusion = f32[16,1024]{1,0:T(8,128)} fusion(f32[16,1024,256]{2,1,0:T(8,128)} %param.7), kind=kLoop, calls=%fused_computation.2 | loop fusion | flops 8372224 | bytes 16842752 | tf_op jit(solution)/shard_map/reduce_sum | solution.py:14
  15.9 12.6 %abs_reduce_fusion.1 = (f32[16,1024]{1,0:T(8,128)}, f32[16,1024]{1,0:T(8,128)}) fusion(f32[16,256,1024]{2,1,0:T(8,128)} %param.6, f32[16,256,1024]{2,1,0:T(8,128)} %param.5), kind=kLoop, calls=%fused_computation.4 | loop fusion | flops 16744448 | bytes 33685504 | tf_op jit(solution)/shard_map/reduce_sum | solution.py:13
  28.5 15.7 %all_gather.3 = bf16[2048,16]{0,1:T(8,128)(2,1)S(1)} all-gather(bf16[256,16]{0,1:T(8,128)(2,1)S(1)} %multiply_convert_fusion), channel_id=1, replica_groups=mesh['owner'=4,'rows'=8] {'rows'}, dimensions={0}, use_global_device_ids=true | all-gather | bytes 73728 | tf_op jit(solution)/shard_map/all_gather | solution.py:41
  44.2 0.7 stack.2
  44.9 3.7 all-to-all-start.3
  48.6 17.6 %copy.19 = f32[16,256,1024]{1,0,2:T(8,128)} copy(f32[16,256,1024]{2,1,0:T(8,128)} %param.6) | data formatting | bytes 33554432 | tf_op args[1]
  66.2 20.6 %all-reduce.3.cloned.1.call-done = (f32[16,1024]{1,0:T(8,128)}, f32[16,1024]{1,0:T(8,128)}, f32[16,1024]{1,0:T(8,128)}) async-done(((f32[16,1024]{1,0:T(8,128)}, f32[16,1024]{1,0:T(8,128)}, f32[16,1024]{1,0:T(8,128)}), (f32[16,1024]{1,0:T(8,128)}, f32[16,1024]{1,0:T(8,128)}, f32[16,1024]{1,0:T(8,128)})) %all-reduce.3.cloned.1.call-update) | async-done | bytes 196624 | tf_op jit(solution)/shard_map/psum | solution.py:10
  86.8 0.8 broadcast_multiply_fusion.1
  87.8 9.6 %divide_convert_fusion = bf16[16,256,1024]{1,0,2:T(8,128)(2,1)} fusion(f32[16,256,1024]{1,0,2:T(8,128)} %copy.19, f32[16,1024]{0,1:T(8,128)S(1)} %copy.18), kind=kLoop, calls=%fused_computation.3 | loop fusion | flops 8388608 | bytes 25231360 | tf_op jit(solution)/shard_map/convert_element_type | solution.py:23
  97.5 5.0 all-to-all-start.1
  102.4 17.6 %copy.16 = f32[16,256,1024]{1,0,2:T(8,128)} copy(f32[16,256,1024]{2,1,0:T(8,128)} %param.5) | data formatting | bytes 33554432 | tf_op args[0]
  120.3 9.7 %divide_convert_fusion.1 = bf16[16,256,1024]{1,0,2:T(8,128)(2,1)} fusion(f32[16,256,1024]{1,0,2:T(8,128)} %copy.16, f32[16,1024]{0,1:T(8,128)S(1)} %copy.15), kind=kLoop, calls=%fused_computation.5 | loop fusion | flops 8388608 | bytes 25231360 | tf_op jit(solution)/shard_map/convert_element_type | solution.py:22
  130.0 156.3 %all-to-all-done.1 = bf16[16,256,1024]{1,0,2:T(8,128)(2,1)} async-done(((bf16[16,256,1024]{1,0,2:T(8,128)(2,1)}), bf16[16,256,1024]{1,0,2:T(8,128)(2,1)}, u32[]{:S(2)}, u32[]{:S(2)}) %all-to-all-start.1) | async-done | bytes 8388640 | tf_op jit(solution)/shard_map/all_to_all | solution.py:28
  286.3 4.9 all-to-all-start
  291.5 16.6 %fusion = bf16[16,1024,256]{2,0,1:T(8,128)(2,1)} fusion(f32[16,1024,256]{2,1,0:T(8,128)} %param.7, f32[16,1024]{0,1:T(8,128)S(1)} %copy.21), kind=kLoop, calls=%fused_computation.1 | loop fusion | flops 8388608 | bytes 25231360 | tf_op jit(solution)/shard_map/convert_element_type | solution.py:24
  308.1 167.0 %all-to-all-done = bf16[16,256,1024]{1,0,2:T(8,128)(2,1)} async-done(((bf16[16,256,1024]{1,0,2:T(8,128)(2,1)}), bf16[16,256,1024]{1,0,2:T(8,128)(2,1)}, u32[]{:S(2)}, u32[]{:S(2)}) %all-to-all-start) | async-done | bytes 8388640 | tf_op jit(solution)/shard_map/all_to_all | solution.py:27
  475.1 5.2 all-to-all-start.2
  480.3 0.6 constant_dynamic-slice_fusion
  482.1 12.3 %copy.20 = bf16[16,8,256,128]{3,2,1,0:T(8,128)(2,1)} copy(bf16[16,8,256,128]{2,0,3,1:T(8,128)(2,1)} %bitcast.4) | data formatting | bytes 16777216 | tf_op jit(solution)/shard_map/all_to_all | solution.py:28
  494.4 12.3 %copy.17 = bf16[16,8,256,128]{3,2,1,0:T(8,128)(2,1)} copy(bf16[16,8,256,128]{2,0,3,1:T(8,128)(2,1)} %bitcast.1) | data formatting | bytes 16777216 | tf_op jit(solution)/shard_map/all_to_all | solution.py:27
  506.7 157.3 %all-to-all-done.2 = bf16[16,1024,256]{2,0,1:T(8,128)(2,1)} async-done(((bf16[16,1024,256]{2,0,1:T(8,128)(2,1)}), bf16[16,1024,256]{2,0,1:T(8,128)(2,1)}, u32[]{:S(2)}, u32[]{:S(2)}) %all-to-all-start.2) | async-done | bytes 8388640 | tf_op jit(solution)/shard_map/all_to_all | solution.py:30
  664.0 11.4 %copy.23 = bf16[16,128,8,256]{3,2,1,0:T(8,128)(2,1)} copy(bf16[16,128,8,256]{3,0,1,2:T(8,128)(2,1)} %bitcast.7) | data formatting | bytes 16777216 | tf_op jit(solution)/shard_map/all_to_all | solution.py:30
  675.4 13.4 %all_to_all.53 = bf16[16,128,2048]{2,1,0:T(8,128)(2,1)} reshape(bf16[16,128,8,256]{3,2,1,0:T(8,128)(2,1)} %copy.23) | data formatting | bytes 16777216 | tf_op jit(solution)/shard_map/all_to_all | solution.py:30
  688.8 0.7 copy.31
  (19 shorter events, 1.9 us)
Async XLA Ops:
  7.2 79.6 %all-reduce.3.cloned.1.call-start = ((), (), s32[]{:S(2)}) async-start(), calls=%async_computation.4 | async-start | bytes 393216 | tf_op jit(solution)/shard_map/psum | solution.py:10
  15.8 12.6 %copy-start.2 = (f32[256,16]{0,1:T(8,128)S(1)}, f32[256,16]{0,1:T(8,128)}, u32[]{:S(2)}) copy-start(f32[256,16]{0,1:T(8,128)} %param.8) | copy-start | bytes 49156
  15.8 12.6 %copy-start.3 = (f32[256]{0:T(256)S(1)}, f32[256]{0:T(256)}, u32[]{:S(2)}) copy-start(f32[256]{0:T(256)} %param.9) | copy-start | bytes 3076
  44.9 52.6 %all-to-all-start.3 = ((bf16[4,2048,16]{1,2,0:T(8,128)(2,1)}), bf16[4,2048,16]{1,2,0:T(8,128)(2,1)S(1)}, u32[]{:S(2)}, u32[]{:S(2)}) async-start(bf16[4,2048,16]{1,2,0:T(8,128)(2,1)} %stack.2), calls=%async_computation.3 | async-start | bytes 524288 | tf_op jit(solution)/shard_map/all_to_all | solution.py:43
  97.5 188.8 %all-to-all-start.1 = ((bf16[16,256,1024]{1,0,2:T(8,128)(2,1)}), bf16[16,256,1024]{1,0,2:T(8,128)(2,1)}, u32[]{:S(2)}, u32[]{:S(2)}) async-start(bf16[16,256,1024]{1,0,2:T(8,128)(2,1)} %divide_convert_fusion), calls=%async_computation.1 | async-start | bytes 16777216 | tf_op jit(solution)/shard_map/all_to_all | solution.py:28
  102.4 17.6 %copy-start.1 = (f32[16,1024]{1,0:T(8,128)S(1)}, f32[16,1024]{1,0:T(8,128)}, u32[]{:S(2)}) copy-start(f32[16,1024]{1,0:T(8,128)} %get-tuple-element.7) | copy-start | bytes 196612
  120.3 171.0 %copy-start = (f32[16,1024]{1,0:T(8,128)S(1)}, f32[16,1024]{1,0:T(8,128)}, u32[]{:S(2)}) copy-start(f32[16,1024]{1,0:T(8,128)} %get-tuple-element.9) | copy-start | bytes 196612
  286.3 188.8 %all-to-all-start = ((bf16[16,256,1024]{1,0,2:T(8,128)(2,1)}), bf16[16,256,1024]{1,0,2:T(8,128)(2,1)}, u32[]{:S(2)}, u32[]{:S(2)}) async-start(bf16[16,256,1024]{1,0,2:T(8,128)(2,1)} %divide_convert_fusion.1), calls=%async_computation | async-start | bytes 16777216 | tf_op jit(solution)/shard_map/all_to_all | solution.py:27
  475.1 188.9 %all-to-all-start.2 = ((bf16[16,1024,256]{2,0,1:T(8,128)(2,1)}), bf16[16,1024,256]{2,0,1:T(8,128)(2,1)}, u32[]{:S(2)}, u32[]{:S(2)}) async-start(bf16[16,1024,256]{2,0,1:T(8,128)(2,1)} %fusion), calls=%async_computation.2 | async-start | bytes 16777216 | tf_op jit(solution)/shard_map/all_to_all | solution.py:30
Sparse Core Ops, SparseCore 0:
  28.6 58.1 all-reduce.2
